TPU v7x, 32 devices: a whole 2x2x4 slice. The times are simulated.
32 devices in a mesh: expert: 4 (over y, x), rep: 4 (over z), hid: 2 (over core).
Axes of the slice: x: 2, y: 2, z: 4, core: 2. Of those that a mesh axis runs over, the one named last changes fastest.
Arguments:
- calib_rows: bfloat16 [8192, 6144], P(('expert', 'rep'), 'hid'), may hold values from -6 to 6
- routes: int32 [8192, 2], P(('expert', 'rep')), may hold values from 0 to 7, all different within a row; in each aligned block of 512 rows (0 to 511, 512 to 1023, ...) at most 256 rows name the same one
- sketch_seed: int32 [6144, 512], P('hid'), may hold values from -1 to 1
- up_weight: bfloat16 [8, 6144, 16384], P('expert', 'hid', 'rep'), may hold values from -0.078125 to 0.078125
Outputs:
- projected: float32 [16384, 8, 512], P(('rep', 'hid'), 'expert')
Inputs may be any that keep to these rules, and one draw needn't show every extreme that they name: `routes`: each row names 2 different experts. In each aligned block of 512 rows no expert is named by more than 256 rows, and every expert is named somewhere.
All inputs are finite; a program needn't handle non-finite values.
Results may differ from a plain program's by a relative error of at most 0.0037.
Values may be sent and summed in bfloat16 or wider, within the bound.
No kernel may reach another device: no remote copies, remote signals or barrier semaphores. Data moves between devices by JAX's collectives and lax.ppermute only.
A program may use at most 192 MiB of HBM per device.

v0:
```python
import jax
import jax.numpy as jnp
from jax import lax
from jax.sharding import PartitionSpec as P

D = 6144
EXPERTS = 8
CAP = 256
damping = 0.25


def shards(calib_rows, routes, sketch_seed, up_weight):
    exp_local = up_weight.shape[0]
    signs_half = sketch_seed.astype(jnp.bfloat16)
    signs_full = sketch_seed.astype(jnp.float32)
    expert_ids = jnp.arange(EXPERTS, dtype=jnp.int32)
    member = jnp.sum((routes[:, :, None] == expert_ids[None, None, :]).astype(jnp.float32), axis=1)
    row_squares = jnp.sum(jnp.square(calib_rows.astype(jnp.float32)), axis=1)
    leader = (lax.axis_index("hid") == 0).astype(jnp.float32)
    counts, squares = lax.psum(
        (jnp.sum(member, axis=0) * leader, jnp.sum(member * row_squares[:, None], axis=0)),
        ("expert", "rep", "hid"),
    )
    flat_routes = routes.reshape(-1)
    one_hot = (flat_routes[:, None] == expert_ids[None, :]).astype(jnp.int32)
    before = jnp.cumsum(one_hot, axis=0) - one_hot
    slot_index = jnp.sum(before * one_hot, axis=1)
    repeated = jnp.repeat(calib_rows, routes.shape[1], axis=0)
    outgoing = jnp.zeros((EXPERTS, CAP, calib_rows.shape[1]), jnp.bfloat16)
    outgoing = outgoing.at[flat_routes, slot_index].set(repeated)
    outgoing = outgoing.reshape(lax.axis_size("expert"), exp_local, CAP, calib_rows.shape[1])
    rows_here = lax.all_to_all(outgoing, "expert", split_axis=0, concat_axis=2, tiled=True)[0]
    partial_value = jnp.einsum(
        "kmd,dr->kmr", rows_here, signs_half, preferred_element_type=jnp.float32
    )
    summed_rows = lax.psum(partial_value, "hid")
    masked = summed_rows.astype(jnp.bfloat16)
    partial_gram = jnp.einsum("kmd,kmr->kdr", rows_here, masked, preferred_element_type=jnp.float32)
    summed = lax.psum(partial_gram, "rep")
    first_expert = lax.axis_index("expert") * exp_local
    row_counts = lax.dynamic_slice_in_dim(counts, first_expert, exp_local)
    square_sums = lax.dynamic_slice_in_dim(squares, first_expert, exp_local)
    ridge = damping * square_sums / (row_counts * D)
    sketch = (
        summed / row_counts[:, None, None] + ridge[:, None, None] * signs_full[None, :, :]
    ).astype(jnp.bfloat16)
    return lax.psum_scatter(
        jnp.einsum("edf,edr->fer", up_weight, sketch, preferred_element_type=jnp.float32),
        "hid",
        scatter_dimension=0,
        tiled=True,
    )


def solution(mesh):
    in_specs = (
        P(("expert", "rep"), "hid"),
        P(("expert", "rep"), None),
        P("hid", None),
        P("expert", "hid", "rep"),
    )
    out_specs = P(("rep", "hid"), "expert", None)
    return jax.shard_map(shards, mesh=mesh, in_specs=in_specs, out_specs=out_specs, check_vma=False)
```

profile of v0, /device:TPU:0, one launch (start us, length us, event | category | flops | bytes accessed | tf_op | source)
XLA Modules:
  0.0 748.2 jit_solution(2252918654287226031)
XLA Ops:
  6.5 0.0 all-reduce.4.cloned.1.call-start
  6.5 0.8 copy.22
  7.4 0.2 eq.45
  7.5 0.2 eq.41
  7.7 0.2 reshape.73
  7.9 2.3 reduce-window.6
  10.2 0.3 slice_reduce_fusion
  10.5 0.2 reduce-window.9
  10.6 0.1 add_bitcast_fusion
  10.7 0.8 and_reduce_fusion
  11.5 0.7 multiply_reduce_fusion.2
  12.2 7.0 broadcast_in_dim.5
  19.3 13.6 %reshape.84 = bf16[1024,3072]{1,0:T(8,128)(2,1)} reshape(bf16[512,2,3072]{2,1,0:T(2,128)(2,1)} %broadcast_in_dim.5) | data formatting | bytes 12582912 | tf_op jit(solution)/shard_map/reshape | solution.py:28
  32.9 17.2 %scatter_custom_fusion = bf16[2048,3072]{1,0:T(8,128)(2,1)} fusion(s32[1024]{0:T(1024)S(1)} %broadcast_select_fusion, bf16[1024,3072]{1,0:T(8,128)(2,1)} %reshape.84, bf16[]{:T(256)} %constant.10.clone.1), kind=kCustom, calls=%fused_computation.3 | custom fusion | bytes 12583424
  50.0 0.0 slice-start
  50.0 144.0 %all_to_all.15 = bf16[4,2,256,3072]{3,2,1,0:T(8,128)(2,1)S(1)} all-to-all(bf16[4,2,256,3072]{3,2,1,0:T(8,128)(2,1)} %bitcast.35), channel_id=1, replica_groups=mesh['expert'=4,'rep'=4,'hid'=2] {'expert'}, dimensions={0} | all-to-all | bytes 25165824 | tf_op jit(solution)/shard_map/all_to_all | solution.py:32
  194.0 0.0 slice-start.1
  194.0 2.3 copy.25
  196.3 0.0 copy-start
  196.3 4.5 copy-done
  200.8 0.0 slice-done
  200.8 0.0 slice-done.1
  200.8 8.8 %fusion.5 = f32[2,1024,512]{2,1,0:T(8,128)} fusion(bf16[2,1024,3072]{2,1,0:T(8,128)(2,1)S(1)} %bitcast.37, s32[3072,512]{1,0:T(8,128)S(1)} %bitcast.40), kind=kOutput, calls=%fused_computation.9 | convolution fusion | flops 6444023808 | bytes 23068672 | tf_op jit(solution)/shard_map/kmd,dr->kmr/dot_general | solution.py:33
  209.6 14.9 %all-reduce.5 = bf16[2,1024,512]{2,1,0:T(8,128)(2,1)S(1)} all-reduce(f32[2,1024,512]{2,1,0:T(8,128)} %fusion.5), channel_id=1, replica_groups=mesh['expert'=4,'rep'=4,'hid'=2] {'hid'}, use_global_device_ids=true, to_apply=%region_4.0 | all-reduce | flops 1048576 | bytes 6291456 | tf_op jit(solution)/shard_map/psum | solution.py:36
  224.5 12.4 %fusion.14 = f32[2,3072,512]{2,1,0:T(8,128)} fusion(bf16[2,1024,3072]{2,1,0:T(8,128)(2,1)} %bitcast.38, bf16[2,1024,512]{2,1,0:T(8,128)(2,1)S(1)} %all-reduce.5), kind=kOutput, calls=%fused_computation.35 | convolution fusion | flops 6442450944 | bytes 27262976 | tf_op jit(solution)/shard_map/kmd,kmr->kdr/dot_general | solution.py:38
  236.9 0.0 copy-start.2
  236.9 0.0 copy-start.1
  236.9 0.0 all-reduce.4.cloned.1.call-update
  236.9 0.0 reduce-scatter.2.cloned.1.call-start
  237.0 0.6 copy-done.2
  237.6 0.1 convert_reduce_fusion
  237.7 1.1 copy-done.1
  238.8 0.7 multiply_reduce_fusion
  239.5 0.1 multiply_reduce_fusion.1
  239.6 44.5 %all-reduce = (f32[8]{0:T(128)S(1)}, f32[8]{0:T(128)S(1)}) all-reduce(f32[8]{0:T(128)S(1)} %broadcast_multiply_fusion, f32[8]{0:T(128)S(1)} %multiply_reduce_fusion.1), channel_id=1, replica_groups=mesh['expert'=4,'rep'=4,'hid'=2] {'expert','rep','hid'}, use_global_device_ids=true, to_apply=%region_7.8 | all-reduce | flops 16 | bytes 128 | tf_op jit(solution)/shard_map/psum | solution.py:20
  284.1 6.3 convert_element_type.35
  290.3 0.1 multiply_divide_fusion
  290.4 373.7 %all-reduce.4.cloned.1.call-done = f32[2,3072,512]{2,1,0:T(8,128)} async-done(((f32[2,3072,512]{2,1,0:T(8,128)}), f32[2,3072,512]{2,1,0:T(8,128)}) %all-reduce.4.cloned.1.call-update) | async-done | bytes 12582928 | tf_op jit(solution)/shard_map/psum | solution.py:39
  664.2 40.0 %convolution_bitcast_fusion = f32[4096,2,512]{0,2,1:T(8,128)} fusion(bf16[2,3072,4096]{2,1,0:T(8,128)(2,1)} %param.7, f32[2,3072,512]{2,1,0:T(8,128)} %all-reduce.4.cloned.1.call-done, f32[3072,512]{1,0:T(8,128)} %convert_element_type.35, f32[2]{0:T(128)S(1)} %get-tuple-element.9, f32[2]{0:T(128)S(1)} %get-tuple-element.10), kind=kOutput, calls=%fused_computation.2 | convolution fusion | flops 25782386688 | bytes 85983248 | tf_op jit(solution)/shard_map/edf,edr->fer/dot_general | solution.py:48
  704.1 0.0 reduce-scatter.2.cloned.1.call-update
  704.2 24.0 %reduce-scatter.2.cloned.1.call-done = f32[2048,2,512]{0,2,1:T(8,128)} async-done(((f32[4096,2,512]{0,2,1:T(8,128)}), f32[2048,2,512]{0,2,1:T(8,128)}) %reduce-scatter.2.cloned.1.call-update) | async-done | bytes 8388624 | tf_op jit(solution)/shard_map/reduce_scatter | solution.py:47
  728.2 13.1 %copy.28 = f32[2048,2,512]{2,1,0:T(2,128)} copy(f32[2048,2,512]{0,2,1:T(8,128)} %reduce-scatter.2.cloned.1.call-done) | data formatting | bytes 16777216 | tf_op jit(solution)/shard_map/reduce_scatter | solution.py:47
  (6 shorter events, 0.1 us)
Async XLA Ops:
  6.5 657.6 %all-reduce.4.cloned.1.call-start = ((), (), s32[]{:S(2)}) async-start(), calls=%async_computation.2 | async-start | bytes 25165824 | tf_op jit(solution)/shard_map/psum | solution.py:39
  50.0 150.7 %slice-start = ((s8[6291456]{0:T(1024)(128)(4,1)}), s8[4194304]{0:T(1024)(128)(4,1)S(1)}, s32[]{:S(2)}) async-start(s8[6291456]{0:T(1024)(128)(4,1)} %bitcast.39), calls=%async_computation.4 | async-start | bytes 8388608
  194.0 6.8 slice-start.1
  196.3 4.5 copy-start
  236.9 0.7 copy-start.2
  236.9 1.9 copy-start.1
  236.9 491.3 %reduce-scatter.2.cloned.1.call-start = ((), (), s32[]{:S(2)}) async-start(), calls=%async_computation.3 | async-start | bytes 25165824 | tf_op jit(solution)/shard_map/reduce_scatter | solution.py:47
Sparse Core Ops, SparseCore 0:
  237.0 427.0 all-reduce.3
  704.3 23.8 reduce-scatter.1
where the time goes:
time: 749 us; the launch traced here: 748 us
  waiting for transfers between devices  398 us (53%)
  blocking collectives  203 us (27%)
  matrix products  61.2 us (8%)
  local copies, waits for them, and re-layouts  61 us (8%)
  between operations  13.5 us (2%)
  other arithmetic  11.3 us (2%)
    psum x1, waiting for transfers between devices, shards(): summed = lax.psum(partial_gram, 'rep')  374 us
    all_to_all x1, blocking collectives, shards(): lax.all_to_all(outgoing, 'expert', split_axis=0, concat_axis=2, tiled=True)  144 us
    psum x1, blocking collectives, shards(): lax.psum((jnp.sum(member, axis=0) * leader, jnp.sum(member * row_squares[...  44.5 us
    dot_general x1, matrix products, shards(): jnp.einsum('edf,edr->fer', up_weight, sketch, preferred_element_type=jnp....  40 us
    unnamed x12, local copies, waits for them, and re-layouts  24.1 us
    reduce_scatter x1, waiting for transfers between devices, shards(): lax.psum_scatter(jnp.einsum('edf,edr->fer', up_weight, sketch, preferred_...  24 us
  transfers between devices with their start and end apart: 2, of which 2 were waited for; matrix products, arithmetic and copies ran while one was open for 1% of the time, Pallas kernels for 0%

commit v1 on v0

--- a/solution.py
+++ b/solution.py
@@ -2,11 +2,16 @@
 import jax.numpy as jnp
 from jax import lax
 from jax.sharding import PartitionSpec as P
+from jax.lax import all_gather
 
 D = 6144
 EXPERTS = 8
 CAP = 256
 damping = 0.25
+
+
+def divide_domain_here(q_in):
+    return jnp.sum(all_gather(q_in, "rep"), axis=0)
 
 
 def shards(calib_rows, routes, sketch_seed, up_weight):
@@ -36,7 +41,7 @@
     summed_rows = lax.psum(partial_value, "hid")
     masked = summed_rows.astype(jnp.bfloat16)
     partial_gram = jnp.einsum("kmd,kmr->kdr", rows_here, masked, preferred_element_type=jnp.float32)
-    summed = lax.psum(partial_gram, "rep")
+    summed = divide_domain_here(partial_gram)
     first_expert = lax.axis_index("expert") * exp_local
     row_counts = lax.dynamic_slice_in_dim(counts, first_expert, exp_local)
     square_sums = lax.dynamic_slice_in_dim(squares, first_expert, exp_local)

time: 749 us -> 1180 us (1.58)
  waiting for transfers between devices: 398 us -> 782 us
  blocking collectives: 203 us -> 228 us
  other arithmetic: 11.3 us -> 35.6 us
    all_gather x0 -> x1, waiting for transfers between devices: none -> 758 us  [divide_domain_here(): return jnp.sum(all_gather(q_in, 'rep'), axis=0)]
    psum x1 -> x0, waiting for transfers between devices: 374 us -> none  [shards(): summed = lax.psum(partial_gram, 'rep')]
    psum x1, blocking collectives: 44.5 us -> 69.3 us  [shards(): lax.psum((jnp.sum(member, axis=0) * leader, jnp.sum(member * row_squares[...]
    reduce_sum x0 -> x1, other arithmetic: none -> 24.2 us  [divide_domain_here(): return jnp.sum(all_gather(q_in, 'rep'), axis=0)]
where the time goes in v1:
time: 1180 us
  waiting for transfers between devices  782 us (66%)
  blocking collectives  228 us (19%)
  local copies, waits for them, and re-layouts  61.1 us (5%)
  matrix products  61.1 us (5%)
  other arithmetic  35.6 us (3%)
  between operations  13.5 us (1%)
    all_gather x1, waiting for transfers between devices, divide_domain_here(): return jnp.sum(all_gather(q_in, 'rep'), axis=0)  758 us
    all_to_all x1, blocking collectives, shards(): lax.all_to_all(outgoing, 'expert', split_axis=0, concat_axis=2, tiled=True)  144 us
    psum x1, blocking collectives, shards(): lax.psum((jnp.sum(member, axis=0) * leader, jnp.sum(member * row_squares[...  69.3 us
    dot_general x1, matrix products, shards(): jnp.einsum('edf,edr->fer', up_weight, sketch, preferred_element_type=jnp....  40 us
    unnamed x12, local copies, waits for them, and re-layouts  24.2 us
    reduce_sum x1, other arithmetic, divide_domain_here(): return jnp.sum(all_gather(q_in, 'rep'), axis=0)  24.2 us
  transfers between devices with their start and end apart: 2, of which 2 were waited for; matrix products, arithmetic and copies ran while one was open for 1% of the time, Pallas kernels for 0%

profile of v1, /device:TPU:0, one launch (start us, length us, event | category | flops | bytes accessed | tf_op | source)
XLA Modules:
  0.0 1181.0 jit_solution(13498941515432641270)
XLA Ops:
  6.5 0.0 all-gather.3.cloned.1.call-start
  6.5 0.8 copy.23
  7.4 0.2 eq.45
  7.5 0.2 eq.41
  7.7 0.2 reshape.73
  7.9 2.3 reduce-window.6
  10.2 0.3 slice_reduce_fusion
  10.5 0.2 reduce-window.9
  10.6 0.1 add_bitcast_fusion
  10.7 0.7 multiply_reduce_fusion.2
  11.5 0.8 and_reduce_fusion
  12.2 7.0 broadcast_in_dim.5
  19.3 13.6 %reshape.84 = bf16[1024,3072]{1,0:T(8,128)(2,1)} reshape(bf16[512,2,3072]{2,1,0:T(2,128)(2,1)} %broadcast_in_dim.5) | data formatting | bytes 12582912 | tf_op jit(solution)/shard_map/reshape | solution.py:33
  32.9 17.2 %scatter_custom_fusion = bf16[2048,3072]{1,0:T(8,128)(2,1)} fusion(s32[1024]{0:T(1024)S(1)} %broadcast_select_fusion, bf16[1024,3072]{1,0:T(8,128)(2,1)} %reshape.84, bf16[]{:T(256)} %constant.10.clone.1), kind=kCustom, calls=%fused_computation.3 | custom fusion | bytes 12583424
  50.0 0.0 slice-start
  50.0 144.0 %all_to_all.15 = bf16[4,2,256,3072]{3,2,1,0:T(8,128)(2,1)S(1)} all-to-all(bf16[4,2,256,3072]{3,2,1,0:T(8,128)(2,1)} %bitcast.36), channel_id=1, replica_groups=mesh['expert'=4,'rep'=4,'hid'=2] {'expert'}, dimensions={0} | all-to-all | bytes 25165824 | tf_op jit(solution)/shard_map/all_to_all | solution.py:37
  194.0 0.0 slice-start.1
  194.0 2.3 copy.26
  196.3 0.0 copy-start
  196.3 4.6 copy-done
  200.9 0.0 slice-done
  200.9 0.0 slice-done.1
  200.9 8.8 fusion.5
  209.7 14.9 %all-reduce.2 = bf16[2,1024,512]{2,1,0:T(8,128)(2,1)S(1)} all-reduce(f32[2,1024,512]{2,1,0:T(8,128)} %fusion.5), channel_id=1, replica_groups=mesh['expert'=4,'rep'=4,'hid'=2] {'hid'}, use_global_device_ids=true, to_apply=%region_4.0 | all-reduce | flops 1048576 | bytes 6291456 | tf_op jit(solution)/shard_map/psum | solution.py:41
  224.6 12.3 %fusion.14 = f32[2,3072,512]{2,1,0:T(8,128)} fusion(bf16[2,1024,3072]{2,1,0:T(8,128)(2,1)} %bitcast.39, bf16[2,1024,512]{2,1,0:T(8,128)(2,1)S(1)} %all-reduce.2), kind=kOutput, calls=%fused_computation.35 | convolution fusion | flops 6442450944 | bytes 27262976 | tf_op jit(solution)/shard_map/kmd,kmr->kdr/dot_general | solution.py:43
  236.9 0.0 copy-start.2
  236.9 0.0 copy-start.1
  237.0 0.0 all-gather.3.cloned.1.call-update
  237.0 0.0 reduce-scatter.2.cloned.1.call-start
  237.0 0.6 copy-done.2
  237.6 0.1 convert_reduce_fusion
  237.8 1.1 copy-done.1
  238.9 0.7 multiply_reduce_fusion
  239.5 0.1 multiply_reduce_fusion.1
  239.7 69.3 %all-reduce = (f32[8]{0:T(128)S(1)}, f32[8]{0:T(128)S(1)}) all-reduce(f32[8]{0:T(128)S(1)} %broadcast_multiply_fusion, f32[8]{0:T(128)S(1)} %multiply_reduce_fusion.1), channel_id=1, replica_groups=mesh['expert'=4,'rep'=4,'hid'=2] {'expert','rep','hid'}, use_global_device_ids=true, to_apply=%region_7.8 | all-reduce | flops 16 | bytes 128 | tf_op jit(solution)/shard_map/psum | solution.py:25
  309.0 6.3 convert_element_type.35
  315.3 0.1 multiply_divide_fusion
  315.4 758.1 %all-gather.3.cloned.1.call-done = f32[8,3072,512]{2,1,0:T(8,128)} async-done(((f32[2,3072,512]{2,1,0:T(8,128)}), f32[8,3072,512]{2,1,0:T(8,128)}) %all-gather.3.cloned.1.call-update) | async-done | bytes 50331664 | tf_op jit(solution)/shard_map/all_gather | solution.py:14
  1073.5 24.2 %reduce_sum.58 = f32[2,3072,512]{2,1,0:T(8,128)} reduce(f32[4,2,3072,512]{3,2,1,0:T(8,128)} %bitcast.35, f32[]{:T(128)} %constant.14.clone.1), dimensions={0}, to_apply=%region_5.0 | reduce | flops 9437184 | bytes 62914564 | tf_op jit(solution)/shard_map/reduce_sum | solution.py:14
  1097.7 40.0 %convolution_bitcast_fusion = f32[4096,2,512]{0,2,1:T(8,128)} fusion(bf16[2,3072,4096]{2,1,0:T(8,128)(2,1)} %param.7, f32[2,3072,512]{2,1,0:T(8,128)} %reduce_sum.58, f32[3072,512]{1,0:T(8,128)} %convert_element_type.35, f32[2]{0:T(128)S(1)} %get-tuple-element.9, f32[2]{0:T(128)S(1)} %get-tuple-element.10), kind=kOutput, calls=%fused_computation.2 | convolution fusion | flops 25782386688 | bytes 85983248 | tf_op jit(solution)/shard_map/edf,edr->fer/dot_general | solution.py:53
  1137.7 0.0 reduce-scatter.2.cloned.1.call-update
  1137.7 23.4 %reduce-scatter.2.cloned.1.call-done = f32[2048,2,512]{0,2,1:T(8,128)} async-done(((f32[4096,2,512]{0,2,1:T(8,128)}), f32[2048,2,512]{0,2,1:T(8,128)}) %reduce-scatter.2.cloned.1.call-update) | async-done | bytes 8388624 | tf_op jit(solution)/shard_map/reduce_scatter | solution.py:52
  1161.1 13.1 %copy.29 = f32[2048,2,512]{2,1,0:T(2,128)} copy(f32[2048,2,512]{0,2,1:T(8,128)} %reduce-scatter.2.cloned.1.call-done) | data formatting | bytes 16777216 | tf_op jit(solution)/shard_map/reduce_scatter | solution.py:52
  (6 shorter events, 0.1 us)
Async XLA Ops:
  6.5 1067.0 %all-gather.3.cloned.1.call-start = ((), (), s32[]{:S(2)}) async-start(), calls=%async_computation.3 | async-start | bytes 62914560 | tf_op jit(solution)/shard_map/all_gather | solution.py:14
  50.0 150.8 %slice-start = ((s8[6291456]{0:T(1024)(128)(4,1)}), s8[4194304]{0:T(1024)(128)(4,1)S(1)}, s32[]{:S(2)}) async-start(s8[6291456]{0:T(1024)(128)(4,1)} %bitcast.40), calls=%async_computation.4 | async-start | bytes 8388608
  194.0 6.9 slice-start.1
  196.3 4.6 copy-start
  236.9 0.7 copy-start.2
  236.9 1.9 copy-start.1
  237.0 924.1 %reduce-scatter.2.cloned.1.call-start = ((), (), s32[]{:S(2)}) async-start(), calls=%async_computation.2 | async-start | bytes 25165824 | tf_op jit(solution)/shard_map/reduce_scatter | solution.py:52
Sparse Core Ops, SparseCore 0:
  237.1 836.3 all-gather.2
  1137.8 23.2 reduce-scatter.1
